TPU v7x, 256 devices: a whole 4x4x8 slice. The times are simulated.
256 devices in a mesh: tp: 4 (over x), dp: 64 (over z, y, core).
Axes of the slice: x: 4, y: 4, z: 8, core: 2. Of those that a mesh axis runs over, the one named last changes fastest.
Arguments:
- item_query: bfloat16 [8192, 2048], P('dp', 'tp'), may hold values from -20 to 20, as said below
- item_keys: bfloat16 [8192, 4, 2048], P('dp', None, 'tp'), may hold values from -20 to 20
- item_values: bfloat16 [8192, 4, 2048], P('dp', None, 'tp'), may hold values from -6 to 6
- item_out_weight: bfloat16 [2048, 4096], P('tp'), may hold values from -0.125 to 0.125
- item_residual: bfloat16 [8192, 4096], P('dp'), may hold values from -3 to 3
- cite_home: int32 [65536, 1], P('dp'), may hold values from 0 to 63; in each aligned block of 1024 rows (0 to 1023, 1024 to 2047, ...) at most 24 rows name the same one
- cite_row: int32 [65536], P('dp'), may hold values from 0 to 127
- seq_length: int32 [64], P('dp'), may hold values from 1 to 1024, 40960 in all
- user_gain: float32 [4096], replicated, may hold values from 0.1 to 1.9
- user_weight: bfloat16 [4096, 16, 384], P('dp', 'tp'), may hold values from -0.09375 to 0.09375
Outputs:
- user_qkv: bfloat16 [65536, 16, 384], P('dp', 'tp')
Inputs may be any that keep to these rules, and one draw needn't show every extreme that they name: `item_query`: in hidden draws some items' queries equal a multiple of keys at their last two tokens. `cite_home`: among the 1024 positions of one sequence at most 24 cite items of one home device, and some home device is cited exactly 24 times. `seq_length`: some sequence has all 1024 positions live.
All inputs are finite; a program needn't handle non-finite values. No bound on the sum of `seq_length` on one device may be relied on, other than what follows from the above.
Results may differ from a plain program's by a relative error of at most 0.0065.
Values may be sent and summed in bfloat16 or wider, within the bound.
No kernel may reach another device: no remote copies, remote signals or barrier semaphores. Data moves between devices by JAX's collectives and lax.ppermute only.
A program may use at most 128 MiB of HBM per device.

v0:
```python
import math
import jax
import jax.numpy as jnp
from jax import lax
from jax.sharding import PartitionSpec as P

HEAD_DIM = 128


def cut_along(x, dim, size):
    before, after = (x.shape[:dim], x.shape[dim + 1 :])
    return jnp.moveaxis(x.reshape(*before, size, -1, *after), dim, 0)


def sent_and_summed(x, axis, dim):
    parts = cut_along(x, dim, lax.axis_size(axis))
    arrived = lax.all_to_all(parts, axis, split_axis=0, concat_axis=0, tiled=True)
    return arrived.sum(axis=0)


def per_device(
    item_query,
    item_keys,
    item_values,
    item_out_weight,
    item_residual,
    cite_home,
    cite_row,
    seq_length,
    user_gain,
    user_weight,
):
    count_items, width_heads = item_query.shape
    tokens_item = item_keys.shape[1]
    local_heads = width_heads // HEAD_DIM
    queries = item_query.reshape(count_items, local_heads, HEAD_DIM)
    keys_all = item_keys.reshape(count_items, tokens_item, local_heads, HEAD_DIM)
    values_all = item_values.reshape(count_items, tokens_item, local_heads, HEAD_DIM)
    scores = jnp.einsum("ihd,ithd->iht", queries, keys_all, preferred_element_type=jnp.float32) * (
        1.0 / math.sqrt(HEAD_DIM)
    )
    probs = jax.nn.softmax(scores, axis=-1).astype(jnp.bfloat16)
    attended = jnp.einsum("iht,ithd->ihd", probs, values_all, preferred_element_type=jnp.float32)
    attended = attended.astype(jnp.bfloat16).reshape(count_items, width_heads)
    partial_value = jnp.dot(attended, item_out_weight, preferred_element_type=jnp.float32)
    summed = sent_and_summed(partial_value, "tp", 1)
    columns = summed.shape[1]
    own_cols = lax.dynamic_slice_in_dim(item_residual, lax.axis_index("tp") * columns, columns, 1)
    item_vec = (summed + own_cols.astype(jnp.float32)).astype(jnp.bfloat16)
    home_dev = cite_home[:, 0]
    length_seq = home_dev.shape[0]
    devices = lax.axis_size("dp")
    capacity = 3 * length_seq // (2 * devices)
    onehot = (home_dev[:, None] == jnp.arange(devices, dtype=jnp.int32)[None, :]).astype(jnp.int32)
    before = jnp.cumsum(onehot, axis=0) - onehot
    slot_index = jnp.sum(before * onehot, axis=1)
    target = home_dev * capacity + slot_index
    wanted = (
        jnp.zeros((devices * capacity,), jnp.int32)
        .at[target]
        .set(cite_row)
        .reshape(devices, capacity)
    )
    asked = lax.all_to_all(wanted, "dp", split_axis=0, concat_axis=0, tiled=True)
    looked = jnp.take(item_vec, asked.reshape(-1), axis=0).reshape(
        devices, capacity, item_vec.shape[1]
    )
    answers = lax.all_to_all(looked, "dp", split_axis=0, concat_axis=0, tiled=True)
    cited = jnp.take(answers.reshape(devices * capacity, item_vec.shape[1]), target, axis=0)
    cited = lax.all_gather(cited, "tp", axis=1, tiled=True)
    values32 = cited.astype(jnp.float32)
    scale = lax.rsqrt(jnp.mean(values32 * values32, axis=1, keepdims=True) + 1e-05)
    normed = (values32 * scale * user_gain[None, :]).astype(jnp.bfloat16)
    shard_rows, user_heads, triple = user_weight.shape
    weight_flat = user_weight.reshape(shard_rows, user_heads * triple)
    projected = jnp.dot(
        normed,
        lax.all_gather(weight_flat, "dp", axis=0, tiled=True),
        preferred_element_type=jnp.float32,
    )
    live = jnp.arange(length_seq, dtype=jnp.int32) < seq_length[0]
    masked = jnp.where(live[:, None], projected, jnp.zeros_like(projected))
    return masked.astype(jnp.bfloat16).reshape(length_seq, user_heads, triple)


def solution(mesh):
    in_specs = (
        P("dp", "tp"),
        P("dp", None, "tp"),
        P("dp", None, "tp"),
        P("tp", None),
        P("dp", None),
        P("dp", None),
        P("dp"),
        P("dp"),
        P(),
        P("dp", "tp", None),
    )
    out_specs = P("dp", "tp", None)
    return jax.shard_map(
        per_device, mesh=mesh, in_specs=in_specs, out_specs=out_specs, check_vma=False
    )
```

profile of v0, /device:TPU:1, one launch (start us, length us, event | category | flops | bytes accessed | tf_op | source)
XLA Modules:
  0.0 401.7 jit_solution(5603883770292417331)
XLA Ops:
  6.5 0.0 copy-start
  6.5 0.8 fusion.23
  7.3 18.0 %reduce-window.6 = s32[64,8,128]{2,1,0:T(8,128)S(1)} reduce-window(s32[64,8,128]{2,1,0:T(8,128)S(1)} %fusion.23, s32[]{:T(128)} %constant.20.clone.1), window={size=1x1x128 pad=0_0x0_0x127_0}, to_apply=%region_0.0 | reduce-window | flops 8323072 | bytes 524292 | tf_op jit(solution)/shard_map/reduce-window
  25.3 0.1 slice.12
  25.4 0.1 copy.19
  25.6 0.1 copy.20
  25.7 0.1 broadcast_add_fusion
  25.9 0.8 fusion.22
  26.6 0.7 and_reduce_fusion
  27.4 4.5 %scatter_custom_fusion = s32[1536]{0:T(1024)S(1)} fusion(s32[1024]{0:T(1024)S(1)} %bitcast.69, s32[1024]{0:T(1024)} %param.16, s32[]{:T(128)} %constant.20.clone.1), kind=kCustom, calls=%fused_computation.46 | custom fusion | bytes 6656 | tf_op jit(solution)/shard_map/scatter | solution.py:61
  31.8 0.7 all_to_all.12
  32.5 13.1 %all-to-all-start = ((s32[64,1,24]{2,1,0:T(1,128)}), s32[64,1,24]{2,1,0:T(1,128)S(1)}, u32[]{:S(2)}, u32[]{:S(2)}) async-start(s32[64,1,24]{2,1,0:T(1,128)} %bitcast.7), calls=%async_computation | async-start | bytes 65536 | tf_op jit(solution)/shard_map/all_to_all | solution.py:64
  45.7 1.3 reshape.152
  47.0 1.7 fusion.18
  48.7 0.1 copy.25
  48.8 0.1 fusion.15
  48.9 0.2 copy.26
  49.1 0.7 fusion.16
  49.8 0.1 reshape.150
  49.9 6.5 %copy.29 = bf16[4096,512]{1,0:T(8,128)(2,1)} copy(bf16[4096,512]{0,1:T(8,128)(2,1)} %bitcast.59) | data formatting | bytes 8388608 | tf_op jit(solution)/shard_map/dot_general | solution.py:45
  56.4 5.0 %convolution_bitcast_fusion = f32[4,128,1024]{2,1,0:T(8,128)} fusion(bf16[128,512,1]{1,0,2:T(8,128)(2,1)S(1)} %reshape.150, bf16[4,1024,512]{2,1,0:T(8,128)(2,1)} %bitcast.57), kind=kOutput, calls=%fused_computation.16 | convolution fusion | flops 536870912 | bytes 6422528 | tf_op jit(solution)/shard_map/dot_general | solution.py:45
  61.3 0.0 all-to-all-done
  61.3 4.0 %all-to-all-start.1 = ((f32[4,128,1024]{2,1,0:T(8,128)}), f32[4,128,1024]{2,1,0:T(8,128)S(1)}, u32[]{:S(2)}, u32[]{:S(2)}) async-start(f32[4,128,1024]{2,1,0:T(8,128)} %convolution_bitcast_fusion), calls=%async_computation.1 | async-start | bytes 4194304 | tf_op jit(solution)/shard_map/all_to_all | solution.py:17
  65.4 0.6 broadcast.90
  66.0 0.8 reduce.7
  66.7 0.1 reshape.118
  66.9 24.2 %all-to-all-done.1 = f32[4,128,1024]{2,1,0:T(8,128)S(1)} async-done(((f32[4,128,1024]{2,1,0:T(8,128)}), f32[4,128,1024]{2,1,0:T(8,128)S(1)}, u32[]{:S(2)}, u32[]{:S(2)}) %all-to-all-start.1) | async-done | bytes 2097184 | tf_op jit(solution)/shard_map/all_to_all | solution.py:17
  91.1 0.2 reduce_sum.41
  91.3 1.0 add_convert_fusion
  92.3 5.8 %gather_fusion = bf16[1536,1024]{1,0:T(8,128)(2,1)} fusion(bf16[128,1024]{1,0:T(8,128)(2,1)S(1)} %add_convert_fusion, s32[2048]{0:T(1024)S(1)} %pad_clamp_fusion), kind=kCustom, calls=%fused_computation | custom fusion | bytes 6297600 | tf_op jit(solution)/shard_map/jit(_take)/gather | solution.py:65
  98.1 3.3 broadcast_select_fusion
  101.3 11.7 %all-to-all-start.2 = ((bf16[64,24,1024]{2,1,0:T(8,128)(2,1)}), bf16[64,24,1024]{2,1,0:T(8,128)(2,1)}, u32[]{:S(2)}, u32[]{:S(2)}) async-start(bf16[64,24,1024]{2,1,0:T(8,128)(2,1)} %broadcast_select_fusion), calls=%async_computation.2 | async-start | bytes 6291456 | tf_op jit(solution)/shard_map/all_to_all | solution.py:68
  113.0 0.0 all-gather.3.cloned.1.call-start
  113.1 72.3 %all-to-all-done.2 = bf16[64,24,1024]{2,1,0:T(8,128)(2,1)} async-done(((bf16[64,24,1024]{2,1,0:T(8,128)(2,1)}), bf16[64,24,1024]{2,1,0:T(8,128)(2,1)}, u32[]{:S(2)}, u32[]{:S(2)}) %all-to-all-start.2) | async-done | bytes 3145760 | tf_op jit(solution)/shard_map/all_to_all | solution.py:68
  185.4 7.3 %gather_fusion.1 = bf16[1024,1024]{1,0:T(8,128)(2,1)S(1)} fusion(bf16[1536,1024]{1,0:T(8,128)(2,1)} %bitcast.19, s32[1024]{0:T(1024)S(1)} %broadcast_clamp_fusion), kind=kCustom, calls=%fused_computation.1 | custom fusion | bytes 4198400 | tf_op jit(solution)/shard_map/jit(_take)/gather | solution.py:69
  192.7 0.0 copy-start.1
  192.7 1.6 broadcast_select_fusion.1
  194.3 0.0 all-gather.3.cloned.1.call-update
  194.3 0.2 all-gather.5.cloned.1.call-start
  194.5 0.0 copy-done.1
  194.5 0.7 copy.31
  195.2 0.0 all-gather.5.cloned.1.call-update
  195.9 0.0 copy-start.2
  195.9 79.5 %all-gather.3.cloned.1.call-done = bf16[1024,4096]{1,0:T(8,128)(2,1)} async-done(((bf16[1024,1024]{1,0:T(8,128)(2,1)}), bf16[1024,4096]{1,0:T(8,128)(2,1)}) %all-gather.3.cloned.1.call-update) | async-done | bytes 8388624 | tf_op jit(solution)/shard_map/all_gather | solution.py:70
  275.4 5.1 %fusion.2 = f32[1024]{0:T(1024)S(1)} fusion(bf16[1024,4096]{1,0:T(8,128)(2,1)} %all-gather.3.cloned.1.call-done), kind=kLoop, calls=%fused_computation.7 | loop fusion | flops 12581888 | bytes 8392704 | tf_op jit(solution)/shard_map/reduce_sum | solution.py:72
  280.5 88.8 %all-gather.5.cloned.1.call-done = bf16[4096,1536]{1,0:T(8,128)(2,1)} async-done(((bf16[64,1536]{1,0:T(8,128)(2,1)}), bf16[4096,1536]{1,0:T(8,128)(2,1)}) %all-gather.5.cloned.1.call-update) | async-done | bytes 12582928 | tf_op jit(solution)/shard_map/all_gather | solution.py:78
  369.3 19.3 %select_convert_fusion = bf16[1024,1536]{1,0:T(8,128)(2,1)} fusion(bf16[4096,1536]{1,0:T(8,128)(2,1)} %all-gather.5.cloned.1.call-done, bf16[1024,4096]{1,0:T(8,128)(2,1)} %all-gather.3.cloned.1.call-done, f32[4096]{0:T(1024)S(1)} %copy-done.2, f32[1024]{0:T(1024)S(1)} %add_rsqrt_fusion, pred[1024]{0:T(1024)(128)(4,1)S(1)} %iota_compare_fusion.2), kind=kOutput, calls=%fused_computation.13 | convolution fusion | flops 12904824832 | bytes 24138752 | tf_op jit(solution)/shard_map/dot_general | solution.py:76
  388.6 6.2 %reshape.121 = bf16[1024,4,384]{2,1,0:T(4,128)(2,1)} reshape(bf16[1024,1536]{1,0:T(8,128)(2,1)} %select_convert_fusion) | data formatting | bytes 6291456 | tf_op jit(solution)/shard_map/reshape | solution.py:83
  (11 shorter events, 0.1 us)
Async XLA Ops:
  6.5 42.5 %copy-start = (bf16[128,4,512]{2,1,0:T(4,128)(2,1)S(1)}, bf16[128,4,512]{2,1,0:T(4,128)(2,1)}, u32[]{:S(2)}) copy-start(bf16[128,4,512]{2,1,0:T(4,128)(2,1)} %param.12) | copy-start | bytes 1572868
  32.5 28.8 %all-to-all-start = ((s32[64,1,24]{2,1,0:T(1,128)}), s32[64,1,24]{2,1,0:T(1,128)S(1)}, u32[]{:S(2)}, u32[]{:S(2)}) async-start(s32[64,1,24]{2,1,0:T(1,128)} %bitcast.7), calls=%async_computation | async-start | bytes 65536 | tf_op jit(solution)/shard_map/all_to_all | solution.py:64
  61.3 29.7 %all-to-all-start.1 = ((f32[4,128,1024]{2,1,0:T(8,128)}), f32[4,128,1024]{2,1,0:T(8,128)S(1)}, u32[]{:S(2)}, u32[]{:S(2)}) async-start(f32[4,128,1024]{2,1,0:T(8,128)} %convolution_bitcast_fusion), calls=%async_computation.1 | async-start | bytes 4194304 | tf_op jit(solution)/shard_map/all_to_all | solution.py:17
  101.3 84.0 %all-to-all-start.2 = ((bf16[64,24,1024]{2,1,0:T(8,128)(2,1)}), bf16[64,24,1024]{2,1,0:T(8,128)(2,1)}, u32[]{:S(2)}, u32[]{:S(2)}) async-start(bf16[64,24,1024]{2,1,0:T(8,128)(2,1)} %broadcast_select_fusion), calls=%async_computation.2 | async-start | bytes 6291456 | tf_op jit(solution)/shard_map/all_to_all | solution.py:68
  113.0 162.4 %all-gather.3.cloned.1.call-start = ((), (), s32[]{:S(2)}) async-start(), calls=%async_computation.3 | async-start | bytes 10485760 | tf_op jit(solution)/shard_map/all_gather | solution.py:70
  192.7 1.9 copy-start.1
  194.3 175.0 %all-gather.5.cloned.1.call-start = ((), (), s32[]{:S(2)}) async-start(), calls=%async_computation.4 | async-start | bytes 12779520 | tf_op jit(solution)/shard_map/all_gather | solution.py:78
  195.9 173.3 %copy-start.2 = (f32[4096]{0:T(1024)S(1)}, f32[4096]{0:T(1024)}, u32[]{:S(2)}) copy-start(f32[4096]{0:T(1024)} %param.18) | copy-start | bytes 49156
Sparse Core Ops, SparseCore 0:
  194.4 80.9 all-gather.2
  278.1 91.0 all-gather.4
where the time goes:
time: 403 us; the launch traced here: 402 us
  waiting for transfers between devices  265 us (66%)
  local copies, waits for them, and re-layouts  34.3 us (9%)
  other arithmetic  32.5 us (8%)
  starting transfers between devices  29.1 us (7%)
  matrix products  26.7 us (7%)
  between operations  14.3 us (4%)
    all_gather x1, waiting for transfers between devices, per_device(): lax.all_gather(weight_flat, 'dp', axis=0, tiled=True)  88.8 us
    all_gather x1, waiting for transfers between devices, per_device(): cited = lax.all_gather(cited, 'tp', axis=1, tiled=True)  79.5 us
    all_to_all x1, waiting for transfers between devices, per_device(): lax.all_to_all(looked, 'dp', split_axis=0, concat_axis=0, tiled=True)  72.3 us
    all_to_all x1, waiting for transfers between devices, sent_and_summed(): lax.all_to_all(parts, axis, split_axis=0, concat_axis=0, tiled=True)  24.2 us
    dot_general x1, matrix products, per_device(): jnp.dot(normed, lax.all_gather(weight_flat, 'dp', axis=0, tiled=True), pr...  19.3 us
    another operation x3, other arithmetic  18.2 us
    all_to_all x1, starting transfers between devices, per_device(): lax.all_to_all(wanted, 'dp', split_axis=0, concat_axis=0, tiled=True)  13.1 us
    all_to_all x1, starting transfers between devices, per_device(): lax.all_to_all(looked, 'dp', split_axis=0, concat_axis=0, tiled=True)  11.7 us
  transfers between devices with their start and end apart: 5, of which 4 were waited for; matrix products, arithmetic and copies ran while one was open for 6% of the time, Pallas kernels for 0%

commit v1 on v0

--- a/solution.py
+++ b/solution.py
@@ -67,7 +67,21 @@
     )
     answers = lax.all_to_all(looked, "dp", split_axis=0, concat_axis=0, tiled=True)
     cited = jnp.take(answers.reshape(devices * capacity, item_vec.shape[1]), target, axis=0)
-    cited = lax.all_gather(cited, "tp", axis=1, tiled=True)
+    ways, here, step = (lax.axis_size("tp"), lax.axis_index("tp"), cited.shape[1])
+    shape = [n * ways if d == 1 else n for d, n in enumerate(cited.shape)]
+    full = lax.dynamic_update_slice_in_dim(
+        jnp.zeros(shape, cited.dtype), cited, here * step, axis=1
+    )
+    going_up = going_down = cited
+    for far in range(1, ways // 2 + 1):
+        going_up = lax.ppermute(going_up, "tp", [(d, (d + 1) % ways) for d in range(ways)])
+        full = lax.dynamic_update_slice_in_dim(full, going_up, (here - far) % ways * step, axis=1)
+        if 2 * far < ways:
+            going_down = lax.ppermute(going_down, "tp", [(d, (d - 1) % ways) for d in range(ways)])
+            full = lax.dynamic_update_slice_in_dim(
+                full, going_down, (here + far) % ways * step, axis=1
+            )
+    cited = full
     values32 = cited.astype(jnp.float32)
     scale = lax.rsqrt(jnp.mean(values32 * values32, axis=1, keepdims=True) + 1e-05)
     normed = (values32 * scale * user_gain[None, :]).astype(jnp.bfloat16)

time: 403 us -> 336 us (0.83)
  waiting for transfers between devices: 265 us -> 181 us
  local copies, waits for them, and re-layouts: 34.3 us -> 46.2 us
    all_gather x1, waiting for transfers between devices: 88.8 us -> 0.02 us  [per_device(): lax.all_gather(weight_flat, 'dp', axis=0, tiled=True)]
    ppermute x0 -> x3, waiting for transfers between devices: none -> 84.5 us  [the longest x2 84.4 us: per_device(): lax.ppermute(going_up, 'tp', [(d, (d + 1) % ways) for d in range(ways)])]
    all_gather x1 -> x0, waiting for transfers between devices: 79.5 us -> none  [per_device(): cited = lax.all_gather(cited, 'tp', axis=1, tiled=True)]
    dynamic_update_slice x0 -> x3, local copies, waits for them, and re-layouts: none -> 7.8 us  [the longest x2 4.63 us: per_device(): lax.dynamic_update_slice_in_dim(full, going_up, (here - far) % ways * ste...]
    broadcast_in_dim x0 -> x1, local copies, waits for them, and re-layouts: none -> 4.24 us  [per_device(): jnp.zeros(shape, cited.dtype)]
  transfers between devices with their start and end apart: 5 -> 7, of which waited for: 4 -> 4; matrix products, arithmetic and copies ran while one was open for 6% -> 23% of each run, Pallas kernels for 0% -> 0%
where the time goes in v1:
time: 336 us; the launch traced here: 332 us
  waiting for transfers between devices  181 us (54%)
  local copies, waits for them, and re-layouts  46.2 us (14%)
  other arithmetic  33.4 us (10%)
  starting transfers between devices  31.5 us (9%)
  matrix products  25.7 us (8%)
  between operations  14.3 us (4%)
    ppermute x2, waiting for transfers between devices, per_device(): lax.ppermute(going_up, 'tp', [(d, (d + 1) % ways) for d in range(ways)])  84.4 us
    all_to_all x1, waiting for transfers between devices, per_device(): lax.all_to_all(looked, 'dp', split_axis=0, concat_axis=0, tiled=True)  72.4 us
    all_to_all x1, waiting for transfers between devices, sent_and_summed(): lax.all_to_all(parts, axis, split_axis=0, concat_axis=0, tiled=True)  24.3 us
    dot_general x1, matrix products, per_device(): jnp.dot(normed, lax.all_gather(weight_flat, 'dp', axis=0, tiled=True), pr...  19.4 us
    another operation x3, other arithmetic  18.2 us
    all_to_all x1, starting transfers between devices, per_device(): lax.all_to_all(wanted, 'dp', split_axis=0, concat_axis=0, tiled=True)  13.1 us
    all_to_all x1, starting transfers between devices, per_device(): lax.all_to_all(looked, 'dp', split_axis=0, concat_axis=0, tiled=True)  11.6 us
    gather x1, local copies, waits for them, and re-layouts, per_device(): jnp.take(answers.reshape(devices * capacity, item_vec.shape[1]), target,...  7.27 us
  transfers between devices with their start and end apart: 7, of which 4 were waited for; matrix products, arithmetic and copies ran while one was open for 23% of the time, Pallas kernels for 0%

profile of v1, /device:TPU:1, one launch (start us, length us, event | category | flops | bytes accessed | tf_op | source)
XLA Modules:
  0.0 332.1 jit_solution(1955746769567577624)
XLA Ops:
  6.5 1.7 copy.31
  8.2 0.0 all-gather.2.cloned.1.call-update
  8.3 0.7 fusion.23
  9.0 18.0 %reduce-window.6 = s32[64,8,128]{2,1,0:T(8,128)S(1)} reduce-window(s32[64,8,128]{2,1,0:T(8,128)S(1)} %fusion.23, s32[]{:T(128)} %constant.72.clone.1), window={size=1x1x128 pad=0_0x0_0x127_0}, to_apply=%region_0.0 | reduce-window | flops 8323072 | bytes 524292 | tf_op jit(solution)/shard_map/reduce-window
  27.0 0.1 slice.12
  27.1 0.1 copy.19
  27.3 0.1 copy.20
  27.4 0.1 broadcast_add_fusion
  27.5 0.8 fusion.22
  28.3 0.7 and_reduce_fusion
  29.0 4.5 %scatter_custom_fusion = s32[1536]{0:T(1024)S(1)} fusion(s32[1024]{0:T(1024)S(1)} %bitcast.68, s32[1024]{0:T(1024)} %param.16, s32[]{:T(128)} %constant.72.clone.1), kind=kCustom, calls=%fused_computation.46 | custom fusion | bytes 6656 | tf_op jit(solution)/shard_map/scatter | solution.py:61
  33.5 0.7 all_to_all.12
  34.2 13.1 %all-to-all-start = ((s32[64,1,24]{2,1,0:T(1,128)}), s32[64,1,24]{2,1,0:T(1,128)S(1)}, u32[]{:S(2)}, u32[]{:S(2)}) async-start(s32[64,1,24]{2,1,0:T(1,128)} %bitcast.7), calls=%async_computation | async-start | bytes 65536 | tf_op jit(solution)/shard_map/all_to_all | solution.py:64
  47.3 0.0 copy-start.2
  47.4 6.6 %copy.29 = bf16[4096,512]{1,0:T(8,128)(2,1)} copy(bf16[4096,512]{0,1:T(8,128)(2,1)} %bitcast.58) | data formatting | bytes 8388608 | tf_op jit(solution)/shard_map/dot_general | solution.py:45
  53.9 0.1 reshape.152
  54.0 0.7 fusion.18
  54.7 0.1 copy.25
  54.8 0.1 fusion.15
  54.9 0.2 copy.26
  55.1 0.7 fusion.16
  55.8 0.1 reshape.150
  55.9 5.0 %convolution_bitcast_fusion = f32[4,128,1024]{2,1,0:T(8,128)} fusion(bf16[128,512,1]{1,0,2:T(8,128)(2,1)S(1)} %reshape.150, bf16[4,1024,512]{2,1,0:T(8,128)(2,1)} %bitcast.56), kind=kOutput, calls=%fused_computation.16 | convolution fusion | flops 536870912 | bytes 6422528 | tf_op jit(solution)/shard_map/dot_general | solution.py:45
  60.9 4.0 %all-to-all-start.1 = ((f32[4,128,1024]{2,1,0:T(8,128)}), f32[4,128,1024]{2,1,0:T(8,128)S(1)}, u32[]{:S(2)}, u32[]{:S(2)}) async-start(f32[4,128,1024]{2,1,0:T(8,128)} %convolution_bitcast_fusion), calls=%async_computation.1 | async-start | bytes 4194304 | tf_op jit(solution)/shard_map/all_to_all | solution.py:17
  64.9 0.5 broadcast.93
  65.4 0.7 reduce.7
  66.1 0.1 reshape.118
  66.3 24.3 %all-to-all-done.1 = f32[4,128,1024]{2,1,0:T(8,128)S(1)} async-done(((f32[4,128,1024]{2,1,0:T(8,128)}), f32[4,128,1024]{2,1,0:T(8,128)S(1)}, u32[]{:S(2)}, u32[]{:S(2)}) %all-to-all-start.1) | async-done | bytes 2097184 | tf_op jit(solution)/shard_map/all_to_all | solution.py:17
  90.6 0.2 reduce_sum.41
  90.8 1.0 add_convert_fusion
  91.8 5.8 %gather_fusion = bf16[1536,1024]{1,0:T(8,128)(2,1)} fusion(bf16[128,1024]{1,0:T(8,128)(2,1)S(1)} %add_convert_fusion, s32[2048]{0:T(1024)S(1)} %pad_clamp_fusion), kind=kCustom, calls=%fused_computation | custom fusion | bytes 6297600 | tf_op jit(solution)/shard_map/jit(_take)/gather | solution.py:65
  97.6 3.3 %broadcast_select_fusion = bf16[64,24,1024]{2,1,0:T(8,128)(2,1)} fusion(bf16[64,24,1024]{2,1,0:T(8,128)(2,1)} %bitcast.57, pred[64,24]{1,0:T(8,128)(4,1)S(1)} %compare_and_fusion), kind=kLoop, calls=%fused_computation.14 | loop fusion | flops 1572864 | bytes 6292992 | tf_op jit(solution)/shard_map/jit(_take)/select_n | solution.py:65
  100.9 11.6 %all-to-all-start.2 = ((bf16[64,24,1024]{2,1,0:T(8,128)(2,1)}), bf16[64,24,1024]{2,1,0:T(8,128)(2,1)}, u32[]{:S(2)}, u32[]{:S(2)}) async-start(bf16[64,24,1024]{2,1,0:T(8,128)(2,1)} %broadcast_select_fusion), calls=%async_computation.2 | async-start | bytes 6291456 | tf_op jit(solution)/shard_map/all_to_all | solution.py:68
  112.5 72.4 %all-to-all-done.2 = bf16[64,24,1024]{2,1,0:T(8,128)(2,1)} async-done(((bf16[64,24,1024]{2,1,0:T(8,128)(2,1)}), bf16[64,24,1024]{2,1,0:T(8,128)(2,1)}, u32[]{:S(2)}, u32[]{:S(2)}) %all-to-all-start.2) | async-done | bytes 3145760 | tf_op jit(solution)/shard_map/all_to_all | solution.py:68
  184.9 7.3 %gather_fusion.1 = bf16[1024,1024]{1,0:T(8,128)(2,1)S(1)} fusion(bf16[1536,1024]{1,0:T(8,128)(2,1)} %bitcast.19, s32[1024]{0:T(1024)S(1)} %broadcast_clamp_fusion), kind=kCustom, calls=%fused_computation.1 | custom fusion | bytes 4198400 | tf_op jit(solution)/shard_map/jit(_take)/gather | solution.py:69
  192.2 4.2 %broadcast_in_dim.49 = bf16[1024,4096]{1,0:T(8,128)(2,1)} broadcast(bf16[]{:T(256)} %constant.70.clone.1), dimensions={} | broadcast | bytes 8388610 | tf_op jit(solution)/shard_map/broadcast_in_dim | solution.py:73
  196.4 2.5 constant_dynamic-update-slice_fusion.3
  198.9 0.4 collective-permute-start
  199.3 2.3 collective-permute-start.1
  201.6 44.0 %collective-permute-done = bf16[1024,1024]{1,0:T(8,128)(2,1)S(1)} collective-permute-done((bf16[1024,1024]{1,0:T(8,128)(2,1)}, bf16[1024,1024]{1,0:T(8,128)(2,1)S(1)}, u32[]{:S(2)}, u32[]{:S(2)}) %collective-permute-start) | collective-permute-done | bytes 2097184 | tf_op jit(solution)/shard_map/ppermute | solution.py:77
  246.3 1.5 constant_dynamic-update-slice_fusion.2
  247.8 3.2 constant_dynamic-update-slice_fusion.1
  251.0 40.4 %collective-permute-done.2 = bf16[1024,1024]{1,0:T(8,128)(2,1)} collective-permute-done((bf16[1024,1024]{1,0:T(8,128)(2,1)S(1)}, bf16[1024,1024]{1,0:T(8,128)(2,1)}, u32[]{:S(2)}, u32[]{:S(2)}) %collective-permute-start.2) | collective-permute-done | bytes 2097184 | tf_op jit(solution)/shard_map/ppermute | solution.py:77
  291.4 3.1 constant_dynamic-update-slice_fusion
  294.5 5.1 %fusion.2 = f32[1024]{0:T(1024)S(1)} fusion(bf16[1024,4096]{1,0:T(8,128)(2,1)} %constant_dynamic-update-slice_fusion), kind=kLoop, calls=%fused_computation.7 | loop fusion | flops 12581888 | bytes 8392704 | tf_op jit(solution)/shard_map/reduce_sum | solution.py:86
  299.6 0.0 all-gather.2.cloned.1.call-done
  299.7 19.4 %select_convert_fusion = bf16[1024,1536]{1,0:T(8,128)(2,1)} fusion(bf16[4096,1536]{1,0:T(8,128)(2,1)} %all-gather.2.cloned.1.call-done, bf16[1024,4096]{1,0:T(8,128)(2,1)} %constant_dynamic-update-slice_fusion, f32[4096]{0:T(1024)S(1)} %copy-done.3, f32[1024]{0:T(1024)S(1)} %add_rsqrt_fusion, pred[1024]{0:T(1024)(128)(4,1)S(1)} %iota_compare_fusion.2), kind=kOutput, calls=%fused_computation.13 | convolution fusion | flops 12904824832 | bytes 24138752 | tf_op jit(solution)/shard_map/dot_general | solution.py:90
  319.0 6.2 %reshape.121 = bf16[1024,4,384]{2,1,0:T(4,128)(2,1)} reshape(bf16[1024,1536]{1,0:T(8,128)(2,1)} %select_convert_fusion) | data formatting | bytes 6291456 | tf_op jit(solution)/shard_map/reshape | solution.py:97
  (20 shorter events, 0.2 us)
Async XLA Ops:
  6.5 48.5 %copy-start = (bf16[128,4,512]{2,1,0:T(4,128)(2,1)S(1)}, bf16[128,4,512]{2,1,0:T(4,128)(2,1)}, u32[]{:S(2)}) copy-start(bf16[128,4,512]{2,1,0:T(4,128)(2,1)} %param.12) | copy-start | bytes 1572868
  6.5 293.1 %all-gather.2.cloned.1.call-start = ((), (), s32[]{:S(2)}) async-start(), calls=%async_computation.3 | async-start | bytes 12779520 | tf_op jit(solution)/shard_map/all_gather | solution.py:92
  34.2 26.7 %all-to-all-start = ((s32[64,1,24]{2,1,0:T(1,128)}), s32[64,1,24]{2,1,0:T(1,128)S(1)}, u32[]{:S(2)}, u32[]{:S(2)}) async-start(s32[64,1,24]{2,1,0:T(1,128)} %bitcast.7), calls=%async_computation | async-start | bytes 65536 | tf_op jit(solution)/shard_map/all_to_all | solution.py:64
  47.3 6.6 %copy-start.1 = (bf16[128,512]{1,0:T(8,128)(2,1)S(1)}, bf16[128,512]{1,0:T(8,128)(2,1)}, u32[]{:S(2)}) copy-start(bf16[128,512]{1,0:T(8,128)(2,1)} %param.10) | copy-start | bytes 393220
  47.3 6.6 %copy-start.2 = (bf16[128,4,512]{2,1,0:T(4,128)(2,1)S(1)}, bf16[128,4,512]{2,1,0:T(4,128)(2,1)}, u32[]{:S(2)}) copy-start(bf16[128,4,512]{2,1,0:T(4,128)(2,1)} %param.11) | copy-start | bytes 1572868
  60.9 29.7 %all-to-all-start.1 = ((f32[4,128,1024]{2,1,0:T(8,128)}), f32[4,128,1024]{2,1,0:T(8,128)S(1)}, u32[]{:S(2)}, u32[]{:S(2)}) async-start(f32[4,128,1024]{2,1,0:T(8,128)} %convolution_bitcast_fusion), calls=%async_computation.1 | async-start | bytes 4194304 | tf_op jit(solution)/shard_map/all_to_all | solution.py:17
  100.9 84.0 %all-to-all-start.2 = ((bf16[64,24,1024]{2,1,0:T(8,128)(2,1)}), bf16[64,24,1024]{2,1,0:T(8,128)(2,1)}, u32[]{:S(2)}, u32[]{:S(2)}) async-start(bf16[64,24,1024]{2,1,0:T(8,128)(2,1)} %broadcast_select_fusion), calls=%async_computation.2 | async-start | bytes 6291456 | tf_op jit(solution)/shard_map/all_to_all | solution.py:68
  198.9 46.7 %collective-permute-start = (bf16[1024,1024]{1,0:T(8,128)(2,1)}, bf16[1024,1024]{1,0:T(8,128)(2,1)S(1)}, u32[]{:S(2)}, u32[]{:S(2)}) collective-permute-start(bf16[1024,1024]{1,0:T(8,128)(2,1)} %get-tuple-element.6), channel_id=1, source_target_pairs={{0,64},{64,128},{128,192},{192,0},{1,65},{65,129},{129,193},{193,1... | collective-permute-start | bytes 6291464 | tf_op jit(solution)/shard_map/ppermute | solution.py:77
  199.3 48.5 %collective-permute-start.1 = (bf16[1024,1024]{1,0:T(8,128)(2,1)}, bf16[1024,1024]{1,0:T(8,128)(2,1)}, u32[]{:S(2)}, u32[]{:S(2)}) collective-permute-start(bf16[1024,1024]{1,0:T(8,128)(2,1)} %get-tuple-element.6), channel_id=1, source_target_pairs={{0,192},{64,0},{128,64},{192,128},{1,193},{65,1},{129,65},{193,129... | collective-permute-start | bytes 6291464 | tf_op jit(solution)/shard_map/ppermute | solution.py:80
  245.6 45.8 %collective-permute-start.2 = (bf16[1024,1024]{1,0:T(8,128)(2,1)S(1)}, bf16[1024,1024]{1,0:T(8,128)(2,1)}, u32[]{:S(2)}, u32[]{:S(2)}) collective-permute-start(bf16[1024,1024]{1,0:T(8,128)(2,1)S(1)} %collective-permute-done), channel_id=1, source_target_pairs={{0,64},{64,128},{128,192},{192,0},{1,65},{65,129},{129,193},{193,1... | collective-permute-start | bytes 6291464 | tf_op jit(solution)/shard_map/ppermute | solution.py:77
  294.5 5.1 %copy-start.3 = (f32[4096]{0:T(1024)S(1)}, f32[4096]{0:T(1024)}, u32[]{:S(2)}) copy-start(f32[4096]{0:T(1024)} %param.18) | copy-start | bytes 49156
Sparse Core Ops, SparseCore 0:
  10.1 93.7 all-gather.1
